TPU v7x, 512 devices: a whole 4x4x16 slice. The times are simulated.
512 devices in a mesh: grp: 4 (over x), dom: 128 (over z, y, core).
Axes of the slice: x: 4, y: 4, z: 16, core: 2. Of those that a mesh axis runs over, the one named last changes fastest.
Arguments:
- node_state: float32 [65536, 6, 128], P(('grp', 'dom')), may hold values from -6 to 6
- node_dest: int32 [65536], P(('grp', 'dom')), may hold values from 0 to 127, as said below
- seg_nodes: float32 [6, 262144], P(None, ('grp', 'dom')), may hold values from -6 to 6
- seg_conn: int32 [3, 524288], P(None, ('grp', 'dom')), may hold values from 0 to 511
- pair_seg: int32 [512, 4, 32], P(('grp', 'dom')), may hold values from 0 to 7
- pair_slot: int32 [512, 4, 32], P(('grp', 'dom')), may hold values from 0 to 255, as said below
Outputs:
- node_force: float32 [65536, 3, 128], P(('grp', 'dom'))
Inputs may be any that keep to these rules, and one draw needn't show every extreme that they name: `node_dest`: at most 2 blocks of one device name the same contact domain; in every grp row one contact domain receives exactly 2 blocks from every device of that row; every device sends at least one block to the contact domain of its own dom index. `pair_slot`: every entry names a slot d * 2 + k that holds a block: device (r, d) sends more than k blocks to the contact domain.
All inputs are finite; a program needn't handle non-finite values.
Results may differ from a plain program's by a relative error of at most 0.00023.
Values sent between devices are 32-bit elements; how exact they have to be, the bound alone decides.
A program may use at most 64 MiB of HBM per device.

v0:
```python
import jax
import jax.numpy as jnp
from jax import lax
from jax.sharding import Mesh
from jax.sharding import PartitionSpec as P

SEG_BLK = 128
DOM = ("dom_0", "dom_1", "dom_2")
GRP_DOM = ("grp", "dom_0", "dom_1", "dom_2")


time_step = 0.5
stiffness = 0.5
radius_sq = 0.5


def in_blocks(shard, dim, devices):
    dims = shard.shape
    blocks = shard.reshape(*dims[:dim], devices, dims[dim] // devices, *dims[dim + 1 :])
    return jnp.moveaxis(blocks, dim, 0)


def in_order(blocks, dim):
    blocks = jnp.moveaxis(blocks, 0, dim)
    dims = blocks.shape
    return blocks.reshape(*dims[:dim], dims[dim] * dims[dim + 1], *dims[dim + 2 :])


def moved_by_axis(blocks, axes, turns):
    dims = [lax.axis_size(a) for a in axes]
    blocks = blocks.reshape(*dims, *blocks.shape[1:])
    for k in turns:
        blocks = lax.all_to_all(blocks, axes[k], split_axis=k, concat_axis=k, tiled=True)
    return blocks.reshape(-1, *blocks.shape[len(axes) :])


def two_step_exchange(shard, groups, turns, split_dim, concat_dim):
    devices = lax.axis_size(groups[0]) * lax.axis_size(groups[1])
    blocks = in_blocks(shard, split_dim, devices)
    return in_order(moved_by_axis(blocks, groups, turns), concat_dim)


def seg_geometry(corners):
    corner_a = corners[:, 0]
    corner_b = corners[:, 1]
    corner_c = corners[:, 2]
    edge_one = corner_b[0:3] - corner_a[0:3]
    edge_two = corner_c[0:3] - corner_a[0:3]
    normal = 0.5 * jnp.stack(
        [
            edge_one[1] * edge_two[2] - edge_one[2] * edge_two[1],
            edge_one[2] * edge_two[0] - edge_one[0] * edge_two[2],
            edge_one[0] * edge_two[1] - edge_one[1] * edge_two[0],
        ]
    )
    centre = (corner_a[0:3] + corner_b[0:3] + corner_c[0:3]) / 3.0
    motion = (corner_a[3:6] + corner_b[3:6] + corner_c[3:6]) / 3.0
    return jnp.concatenate([normal, centre, motion], axis=0)


def tile_force(node_rows, geometry):
    clearance = jnp.zeros((geometry.shape[1], node_rows.shape[1]), jnp.float32)
    distance = jnp.zeros((geometry.shape[1], node_rows.shape[1]), jnp.float32)
    for axis_id in range(3):
        offset = node_rows[axis_id][None, :] - geometry[3 + axis_id][:, None]
        drift = node_rows[3 + axis_id][None, :] - geometry[6 + axis_id][:, None]
        clearance = clearance + geometry[axis_id][:, None] * (offset + time_step * drift)
        distance = distance + offset * offset
    pressure = stiffness * jnp.exp(-distance / radius_sq) * jnp.maximum(-clearance, 0.0)
    return jnp.dot(
        geometry[0:3], pressure, precision=lax.Precision.HIGHEST, preferred_element_type=jnp.float32
    )


def place_rows(slot_ids, values, slot_total):
    onehot = (slot_ids[None, :] == jnp.arange(slot_total, dtype=jnp.int32)[:, None]).astype(
        jnp.float32
    )
    flattened = values.reshape(values.shape[0], -1)
    placed = jnp.dot(
        onehot, flattened, precision=lax.Precision.HIGHEST, preferred_element_type=jnp.float32
    )
    return placed.reshape((slot_total,) + values.shape[1:])


def shards(node_state, node_dest, seg_nodes, seg_conn, pair_seg, pair_slot):
    dom_count = lax.axis_size(DOM)
    grp_count = lax.axis_size("grp")
    block_count = node_state.shape[0]
    capacity = max(2, 2 * block_count // dom_count)
    slot_count = dom_count * capacity
    order_ids = jnp.arange(block_count, dtype=jnp.int32)
    earlier = order_ids[None, :] < order_ids[:, None]
    same_dom = node_dest[:, None] == node_dest[None, :]
    slot_rank = jnp.sum((same_dom & earlier).astype(jnp.int32), axis=1)
    target_slot = node_dest * capacity + slot_rank
    outgoing = place_rows(target_slot, node_state, slot_count)
    received = two_step_exchange(outgoing, (("dom_0", "dom_1"), "dom_2"), (1, 0), 0, 0)
    corners = jnp.take(seg_nodes, seg_conn, axis=1)
    geometry = seg_geometry(corners)
    seg_blocks = geometry.shape[1] // SEG_BLK
    geo_blocks = jnp.transpose(geometry.reshape(9, seg_blocks, SEG_BLK), (1, 0, 2))
    seg_table = pair_seg[0]
    slot_table = pair_slot[0]
    geo_all = lax.all_gather(geo_blocks, "grp", axis=0, tiled=True)
    seg_in, slot_in = (
        lax.all_to_all(seg_table, "grp", split_axis=0, concat_axis=0, tiled=True),
        lax.all_to_all(slot_table, "grp", split_axis=0, concat_axis=0, tiled=True),
    )
    owner_base = (jnp.arange(grp_count, dtype=jnp.int32) * seg_blocks)[:, None]
    seg_ids = (seg_in + owner_base).reshape(-1)
    slot_ids = slot_in.reshape(-1)
    forces = jax.vmap(tile_force)(
        jnp.take(received, slot_ids, axis=0), jnp.take(geo_all, seg_ids, axis=0)
    )
    own_forces = place_rows(slot_ids, forces, slot_count)
    returned = lax.all_to_all(own_forces, DOM, split_axis=0, concat_axis=0, tiled=True)
    return jnp.take(returned, target_slot, axis=0)


def solution(mesh):
    split = Mesh(
        mesh.devices.reshape(mesh.shape["grp"], 16, 4, 2), ("grp", "dom_0", "dom_1", "dom_2")
    )
    placed = (
        P(GRP_DOM, None, None),
        P(GRP_DOM),
        P(None, GRP_DOM),
        P(None, GRP_DOM),
        P(GRP_DOM, None, None),
        P(GRP_DOM, None, None),
    )
    return jax.shard_map(
        shards, mesh=split, in_specs=placed, out_specs=P(GRP_DOM, None, None), check_vma=False
    )
```

profile of v0, /device:TPU:1, one launch (start us, length us, event | category | flops | bytes accessed | tf_op | source)
XLA Modules:
  0.0 166.9 jit_solution(1052670801400604042)
XLA Ops:
  0.0 0.9 convert_reduce_fusion
  0.9 0.7 compare_and_fusion.3
  1.6 1.2 copy.65
  2.7 0.0 copy-start
  2.8 0.5 fusion.34
  3.3 10.8 %all_to_all.39 = f32[64,2,2,6,128]{4,0,3,2,1:T(8,128)S(1)} all-to-all(f32[64,2,2,6,128]{4,0,3,2,1:T(8,128)S(1)} %fusion.34), channel_id=1, replica_groups=mesh['grp'=4,'dom_0'=16,'dom_1'=4,'dom_2'=2] {'dom_2'}, dimensions={1} | all-to-all | bytes 1572864 | tf_op jit(solution)/shard_map/all_to_all | solution.py:33
  14.1 3.2 %all-to-all-start.1 = ((s32[4,1,32]{2,1,0:T(1,128)}), s32[4,1,32]{2,1,0:T(1,128)S(1)}, u32[]{:S(2)}, u32[]{:S(2)}) async-start(s32[4,1,32]{2,1,0:T(1,128)} %bitcast.4), calls=%async_computation.1 | async-start | bytes 4096 | tf_op jit(solution)/shard_map/all_to_all | solution.py:107
  17.3 0.0 copy-done
  17.4 4.0 %all-to-all-done.1 = s32[4,1,32]{2,1,0:T(1,128)S(1)} async-done(((s32[4,1,32]{2,1,0:T(1,128)}), s32[4,1,32]{2,1,0:T(1,128)S(1)}, u32[]{:S(2)}, u32[]{:S(2)}) %all-to-all-start.1) | async-done | bytes 544 | tf_op jit(solution)/shard_map/all_to_all | solution.py:107
  21.4 3.2 %all-to-all-start = ((s32[4,1,32]{2,1,0:T(1,128)}), s32[4,1,32]{2,1,0:T(1,128)S(1)}, u32[]{:S(2)}, u32[]{:S(2)}) async-start(s32[4,1,32]{2,1,0:T(1,128)} %bitcast.1), calls=%async_computation | async-start | bytes 4096 | tf_op jit(solution)/shard_map/all_to_all | solution.py:108
  24.6 0.0 copy-start.1
  24.6 1.5 copy.66
  26.1 2.5 %all-to-all-done = s32[4,1,32]{2,1,0:T(1,128)S(1)} async-done(((s32[4,1,32]{2,1,0:T(1,128)}), s32[4,1,32]{2,1,0:T(1,128)S(1)}, u32[]{:S(2)}, u32[]{:S(2)}) %all-to-all-start) | async-done | bytes 544 | tf_op jit(solution)/shard_map/all_to_all | solution.py:108
  28.6 13.9 %all-to-all-start.3 = ((f32[64,2,2,6,128]{4,2,3,1,0:T(2,128)}), f32[64,2,2,6,128]{4,2,3,1,0:T(2,128)S(1)}, u32[]{:S(2)}, u32[]{:S(2)}) async-start(f32[64,2,2,6,128]{4,2,3,1,0:T(2,128)} %copy.66), calls=%async_computation.3 | async-start | bytes 1572864 | tf_op jit(solution)/shard_map/all_to_all | solution.py:33
  42.6 0.1 add.137
  42.6 0.1 add.148
  42.7 0.1 add.138
  42.8 0.0 copy-done.1
  42.8 0.1 copy.62
  43.0 8.1 %gather_fusion = f32[3072,6]{1,0:T(8,128)S(1)} fusion(f32[6,512]{0,1:T(8,128)S(1)} %copy.62, s32[3072]{0:T(1024)S(1)} %broadcast_clamp_fusion), kind=kCustom, calls=%fused_computation | custom fusion | bytes 159744 | tf_op jit(solution)/shard_map/jit(_take)/gather | solution.py:99
  51.1 0.5 copy.63
  51.7 10.0 %all_gather.3 = f32[32,9,128]{2,0,1:T(8,128)S(1)} all-gather(f32[8,9,128]{2,0,1:T(8,128)S(1)} %maximum_bitcast_fusion), channel_id=1, replica_groups=mesh['grp'=4,'dom_0'=16,'dom_1'=4,'dom_2'=2] {'grp'}, dimensions={0}, use_global_device_ids=true | all-gather | bytes 184320 | tf_op jit(solution)/shard_map/all_gather | solution.py:105
  61.7 0.1 copy.64
  61.8 0.1 all_to_all.30
  61.9 0.5 broadcast.150
  62.4 0.7 reduce.10
  63.1 0.1 all_to_all.29
  63.2 0.1 reshape.189
  63.3 0.7 reduce.11
  63.9 0.1 eq.61
  64.0 0.8 gather_fusion.1
  64.9 0.2 broadcast_select_fusion
  65.1 0.4 fusion.54
  65.5 15.7 %all-to-all-done.3 = f32[64,2,2,6,128]{4,2,3,1,0:T(2,128)S(1)} async-done(((f32[64,2,2,6,128]{4,2,3,1,0:T(2,128)}), f32[64,2,2,6,128]{4,2,3,1,0:T(2,128)S(1)}, u32[]{:S(2)}, u32[]{:S(2)}) %all-to-all-start.3) | async-done | bytes 786464 | tf_op jit(solution)/shard_map/all_to_all | solution.py:33
  81.2 0.3 copy.67
  81.4 0.5 copy.68
  81.9 0.8 gather_fusion.2
  82.7 0.2 broadcast_select_fusion.1
  82.9 0.3 fusion.55
  83.2 37.2 %fusion.14 = f32[128,3,128]{2,1,0:T(4,128)S(1)} fusion(f32[128,128]{1,0:T(8,128)S(1)} %bitcast.77, f32[128,128]{1,0:T(8,128)S(1)} %bitcast.86, f32[128,128]{1,0:T(8,128)S(1)} %bitcast.78, f32[128,128]{1,0:T(8,128)S(1)} %bitcast.79, f32[128,128]{1,0:T(8,128)S(1)} %bitcast.87, f32[128,128]{1,0:T(8,128)S(1)} %bitcast.80, f32[128,128]{1,0:T(8,128)S(1)} %bitcast.81, ...), kind=kOutput, calls=%fused_computation.24 | convolution fusion | flops 134217728 | bytes 1441792 | tf_op jit(solution)/shard_map/vmap()/dot_general | solution.py:70
  120.4 0.1 copy.69
  120.5 0.3 fusion.37
  120.9 1.1 copy.70
  122.0 12.6 %all-to-all-start.4 = ((f32[256,3,128]{2,1,0:T(4,128)}), f32[256,3,128]{2,1,0:T(4,128)S(1)}, u32[]{:S(2)}, u32[]{:S(2)}) async-start(f32[256,3,128]{2,1,0:T(4,128)} %copy.70), calls=%async_computation.4 | async-start | bytes 1048576 | tf_op jit(solution)/shard_map/all_to_all | solution.py:117
  134.6 30.7 %all-to-all-done.4 = f32[256,3,128]{2,1,0:T(4,128)S(1)} async-done(((f32[256,3,128]{2,1,0:T(4,128)}), f32[256,3,128]{2,1,0:T(4,128)S(1)}, u32[]{:S(2)}, u32[]{:S(2)}) %all-to-all-start.4) | async-done | bytes 393248 | tf_op jit(solution)/shard_map/all_to_all | solution.py:117
  165.2 0.8 gather_fusion.3
  166.0 0.2 broadcast_select_fusion.2
  166.2 0.7 copy.71
  (20 shorter events, 0.2 us)
Async XLA Ops:
  2.7 14.6 %copy-start = (s32[3,1024]{1,0:T(4,128)S(1)}, s32[3,1024]{1,0:T(4,128)}, u32[]{:S(2)}) copy-start(s32[3,1024]{1,0:T(4,128)} %param.9) | copy-start | bytes 36868
  14.1 7.3 %all-to-all-start.1 = ((s32[4,1,32]{2,1,0:T(1,128)}), s32[4,1,32]{2,1,0:T(1,128)S(1)}, u32[]{:S(2)}, u32[]{:S(2)}) async-start(s32[4,1,32]{2,1,0:T(1,128)} %bitcast.4), calls=%async_computation.1 | async-start | bytes 4096 | tf_op jit(solution)/shard_map/all_to_all | solution.py:107
  21.4 7.3 %all-to-all-start = ((s32[4,1,32]{2,1,0:T(1,128)}), s32[4,1,32]{2,1,0:T(1,128)S(1)}, u32[]{:S(2)}, u32[]{:S(2)}) async-start(s32[4,1,32]{2,1,0:T(1,128)} %bitcast.1), calls=%async_computation | async-start | bytes 4096 | tf_op jit(solution)/shard_map/all_to_all | solution.py:108
  24.6 18.2 %copy-start.1 = (f32[6,512]{1,0:T(8,128)S(1)}, f32[6,512]{1,0:T(8,128)}, u32[]{:S(2)}) copy-start(f32[6,512]{1,0:T(8,128)} %param.8) | copy-start | bytes 36868
  28.6 52.5 %all-to-all-start.3 = ((f32[64,2,2,6,128]{4,2,3,1,0:T(2,128)}), f32[64,2,2,6,128]{4,2,3,1,0:T(2,128)S(1)}, u32[]{:S(2)}, u32[]{:S(2)}) async-start(f32[64,2,2,6,128]{4,2,3,1,0:T(2,128)} %copy.66), calls=%async_computation.3 | async-start | bytes 1572864 | tf_op jit(solution)/shard_map/all_to_all | solution.py:33
  122.0 43.3 %all-to-all-start.4 = ((f32[256,3,128]{2,1,0:T(4,128)}), f32[256,3,128]{2,1,0:T(4,128)S(1)}, u32[]{:S(2)}, u32[]{:S(2)}) async-start(f32[256,3,128]{2,1,0:T(4,128)} %copy.70), calls=%async_computation.4 | async-start | bytes 1048576 | tf_op jit(solution)/shard_map/all_to_all | solution.py:117
where the time goes:
time: 169 us; the launch traced here: 167 us
  waiting for transfers between devices  52.8 us (31%)
  matrix products  38.1 us (23%)
  starting transfers between devices  32.9 us (19%)
  blocking collectives  20.9 us (12%)
  local copies, waits for them, and re-layouts  18.2 us (11%)
  other arithmetic  3.67 us (2%)
    dot_general x1, matrix products, tile_force(): jnp.dot(geometry[0:3], pressure, precision=lax.Precision.HIGHEST, preferr...  37.2 us
    all_to_all x1, waiting for transfers between devices, shards(): lax.all_to_all(own_forces, DOM, split_axis=0, concat_axis=0, tiled=True)  30.7 us
    all_to_all x1, waiting for transfers between devices, moved_by_axis(): lax.all_to_all(blocks, axes[k], split_axis=k, concat_axis=k, tiled=True)  15.7 us
    all_to_all x1, starting transfers between devices, moved_by_axis(): lax.all_to_all(blocks, axes[k], split_axis=k, concat_axis=k, tiled=True)  13.9 us
    all_to_all x1, starting transfers between devices, shards(): lax.all_to_all(own_forces, DOM, split_axis=0, concat_axis=0, tiled=True)  12.6 us
    all_to_all x1, blocking collectives, moved_by_axis(): lax.all_to_all(blocks, axes[k], split_axis=k, concat_axis=k, tiled=True)  10.8 us
    all_gather x1, blocking collectives, shards(): geo_all = lax.all_gather(geo_blocks, 'grp', axis=0, tiled=True)  10 us
    gather x2, local copies, waits for them, and re-layouts, shards(): corners = jnp.take(seg_nodes, seg_conn, axis=1)  8.59 us
  transfers between devices with their start and end apart: 4, of which 4 were waited for; matrix products, arithmetic and copies ran while one was open for 8% of the time, Pallas kernels for 0%

commit v1 on v0

v1 whole, which is shorter than its diff:
```python
import functools

import jax
import jax.numpy as jnp
from jax import lax
from jax.experimental import pallas as pl
from jax.experimental.pallas import tpu as pltpu
from jax.sharding import Mesh
from jax.sharding import PartitionSpec as P

AXES = ("grp", "dom_0", "dom_1", "dom_2")
NX, NZ, NY, NC = 4, 16, 4, 2
MESH = pl.DeviceIdType.MESH
REACH = 3
F32 = jnp.float32

time_step = 0.5
stiffness = 0.5
radius_sq = 0.5


def prep_kernel(dest, node, seg_nodes, conn, pseg, pslot, s_out, geo, tgt, cnt):
    z = lax.axis_index("dom_0")

    def clear(i, _):
        cnt[i] = 0
        return 0

    lax.fori_loop(0, 128, clear, 0, unroll=16)

    def place(i, _):
        d = dest[i]
        k = cnt[d]
        cnt[d] = k + 1
        p = d & 7
        slot = (d >> 3) * 2 + k
        s_out[pl.ds(p * 192 + slot, 6, stride=32), :] = node[i]
        tgt[i] = p * 96 + slot
        return 0

    lax.fori_loop(0, 128, place, 0, unroll=8)

    corners = []
    for k in range(3):
        idx = jnp.concatenate([conn[k : k + 1, b * 128 : (b + 1) * 128] for b in range(8)], axis=0)
        hi = lax.shift_right_logical(idx, 7)
        lo = lax.bitwise_and(idx, 127)
        comps = []
        for i in range(6):
            got = None
            for q in range(4):
                table = jnp.broadcast_to(seg_nodes[i : i + 1, q * 128 : (q + 1) * 128], (8, 128))
                part = jnp.take_along_axis(table, lo, axis=1)
                got = part if got is None else jnp.where(hi == q, part, got)
            comps.append(got)
        corners.append(comps)
    a, b, c = corners
    e1 = [b[i] - a[i] for i in range(3)]
    e2 = [c[i] - a[i] for i in range(3)]
    n = [0.5 * (e1[(i + 1) % 3] * e2[(i + 2) % 3] - e1[(i + 2) % 3] * e2[(i + 1) % 3]) for i in range(3)]
    m = [(a[i] + b[i] + c[i]) / 3.0 for i in range(3)]
    u = [(a[i + 3] + b[i + 3] + c[i + 3]) / 3.0 for i in range(3)]
    off = sum(n[i] * (m[i] + time_step * u[i]) for i in range(3))
    for i, v in enumerate(n + m + [off]):
        geo[pl.ds(i, 8, stride=8), :] = v
    shift = (z & 3) * 32
    for base, tab in ((7, pseg), (39, pslot)):
        t = jnp.concatenate([tab[0].astype(F32), jnp.zeros((4, 96), F32)], axis=1)
        geo[pl.ds(base, 4, stride=8), :] = pltpu.roll(t, shift, 1)


def exchange_kernel(s, geo, n_out, g_out, ys, yr, zs, zr, xs, xr):
    g, z = lax.axis_index("grp"), lax.axis_index("dom_0")
    y, c = lax.axis_index("dom_1"), lax.axis_index("dom_2")
    right, left = (g + 1) % NX, (g + 3) % NX

    def zat(k):
        return (z + k + NZ) % NZ

    peers = [(right, z, y, c), (left, z, y, c)]
    for e in range(1, REACH + 1):
        peers += [(g, zat(e), y, c), (g, zat(-e), y, c)]
    turns = [(dy, dc) for dy in range(NY) for dc in range(NC) if dy or dc]
    for dy, dc in turns:
        peers.append((g, z, (y + dy) % NY, (c + dc) % NC))
    barrier = pltpu.get_barrier_semaphore()
    for peer in peers:
        pl.semaphore_signal(barrier, inc=1, device_id=peer, device_id_type=MESH)
    pl.semaphore_wait(barrier, len(peers))

    me = y * 2 + c
    sends = []

    def send(src, dst, ss, rs, dev):
        copy = pltpu.make_async_remote_copy(
            src_ref=src, dst_ref=dst, send_sem=ss, recv_sem=rs, device_id=dev, device_id_type=MESH
        )
        copy.start()
        sends.append(copy)

    def landed(dst, ss, rs, dev):
        pltpu.make_async_remote_copy(
            src_ref=dst, dst_ref=dst, send_sem=ss, recv_sem=rs, device_id=dev, device_id_type=MESH
        ).wait_recv()

    def number(sign, d):
        return 0 if d == 0 else (d if sign > 0 else 8 + d)

    most = {1: 8, -1: 7}

    def forward_z(sign, p, src):
        for e in range(1, REACH + 1):
            if p + e <= most[sign]:
                k = number(sign, p + e) - 1
                send(src, g_out.at[g, zat(-sign * p)], zs.at[k], zr.at[k], (g, zat(sign * e), y, c))

    def spread_x(sign, d, src):
        k = number(sign, d)
        dst = g_out.at[g, zat(-sign * d)]
        send(src, dst, xs.at[k, 0], xr.at[k, 0], (right, z, y, c))
        send(src, dst, xs.at[k, 1], xr.at[k, 1], (left, z, y, c))

    def relay_x(sign, d):
        k = number(sign, d)
        zz = zat(-sign * d)
        landed(g_out.at[left, zz], xs.at[k, 0], xr.at[k, 0], (left, z, y, c))
        if k % 2 == 0:
            send(g_out.at[left, zz], g_out.at[left, zz], xs.at[k, 2], xr.at[k, 2], (right, z, y, c))
        landed(g_out.at[right, zz], xs.at[k, 1], xr.at[k, 1], (right, z, y, c))
        if k % 2 == 1:
            send(g_out.at[right, zz], g_out.at[right, zz], xs.at[k, 2], xr.at[k, 2], (left, z, y, c))

    for sign in (1, -1):
        forward_z(sign, 0, geo)
    spread_x(1, 0, geo)
    for dy, dc in turns:
        k = dy * 2 + dc - 1
        to_y, to_c = (y + dy) % NY, (c + dc) % NC
        send(s.at[to_y * 2 + to_c], n_out.at[me], ys.at[k], yr.at[k], (g, z, to_y, to_c))
    g_out[g, z] = geo[...]
    n_out[me] = s[me]

    order = [(1, 0)]
    for d in range(1, 9):
        order += [(sign, d) for sign in (1, -1) if d <= most[sign]]
    lag = 4
    for i, (sign, d) in enumerate(order):
        if d > 0:
            k = number(sign, d) - 1
            hop = d - ((d - 1) // REACH) * REACH
            slot = g_out.at[g, zat(-sign * d)]
            landed(slot, zs.at[k], zr.at[k], (g, zat(-sign * hop), y, c))
            if d % REACH == 0:
                forward_z(sign, d, slot)
            spread_x(sign, d, slot)
        if i >= lag:
            relay_x(*order[i - lag])
    for item in order[-lag:]:
        relay_x(*item)
    for sign, d in order:
        k = number(sign, d)
        far = (g + 2) % NX
        came = left if k % 2 == 0 else right
        landed(g_out.at[far, zat(-sign * d)], xs.at[k, 2], xr.at[k, 2], (came, z, y, c))
    for dy, dc in turns:
        k = dy * 2 + dc - 1
        fy, fc = (y - dy + NY) % NY, (c + dc) % NC
        landed(n_out.at[fy * 2 + fc], ys.at[k], yr.at[k], (g, z, fy, fc))
    for copy in sends:
        copy.wait_send()


def force_kernel(n_in, g_in, f_out, lists_v, lists, sem):
    r, z = lax.axis_index("grp"), lax.axis_index("dom_0")

    def rows(base):
        got = None
        for q in range(4):
            part = g_in[pl.ds(q * 64 + base, 16, stride=256), :]
            got = part if got is None else got + part
        return got

    seg = rows(r * 8 + 7)
    slot = rows(r * 8 + 39).astype(jnp.int32)
    lane = lax.broadcasted_iota(jnp.int32, (16, 128), 1)
    sub = lax.broadcasted_iota(jnp.int32, (16, 128), 0)
    src = sub * 4 + lax.shift_right_logical(lane, 5)
    hit = lax.shift_right_logical(slot, 4) == z
    mask = jnp.where(hit, 1.0, 0.0).astype(F32)
    code_a = src.astype(F32)
    code_b = seg * 16.0 + lax.bitwise_and(slot, 15).astype(F32)
    i0 = lax.broadcasted_iota(jnp.int32, (128, 128), 0)
    i1 = lax.broadcasted_iota(jnp.int32, (128, 128), 1)
    before = jnp.where(i0 < i1, 1.0, 0.0).astype(F32)
    inner = jnp.dot(mask, before, preferred_element_type=F32)
    total = jnp.dot(mask, jnp.ones((128, 128), F32), preferred_element_type=F32)
    j0 = lax.broadcasted_iota(jnp.int32, (16, 16), 0)
    j1 = lax.broadcasted_iota(jnp.int32, (16, 16), 1)
    above = jnp.dot(jnp.where(j1 < j0, 1.0, 0.0).astype(F32), total, preferred_element_type=F32)
    pos = (inner + above).astype(jnp.int32)
    high = jnp.where(hit, lax.shift_right_logical(pos, 7), -1)
    low = lax.bitwise_and(pos, 127)
    packed = jnp.zeros((32, 128), F32)
    for i in range(16):
        at = high[i : i + 1] == sub
        left = jnp.concatenate(
            [jnp.where(at, code_a[i : i + 1], 0.0), jnp.where(at, code_b[i : i + 1], 0.0)], axis=0
        )
        spot = jnp.where(low[i : i + 1] == i0, 1.0, 0.0).astype(F32)
        packed = packed + lax.dot_general(left, spot, (((1,), (1,)), ((), ())), preferred_element_type=F32)
    lists_v[0:32, :] = packed.astype(jnp.int32)
    lists_v[32:40, :] = jnp.broadcast_to(total[15:16] + above[15:16], (8, 128)).astype(jnp.int32)
    copy = pltpu.make_async_copy(lists_v, lists, sem)
    copy.start()
    f_out[...] = jnp.zeros_like(f_out)
    copy.wait()

    def pair(p, _):
        a = lists[lax.shift_right_logical(p, 7), lax.bitwise_and(p, 127)]
        b = lists[16 + lax.shift_right_logical(p, 7), lax.bitwise_and(p, 127)]
        t = lax.shift_right_logical(b, 4)
        who = lax.bitwise_and(lax.shift_right_logical(b, 1), 7)
        place = lax.bitwise_and(a, 15) * 2 + lax.bitwise_and(b, 1)
        tile = g_in[pl.ds(pl.multiple_of(a * 64 + t * 8, 8), 8), :]
        node = n_in[pl.ds(who * 192 + place, 6, stride=32), :]
        cols = tile.T
        clear = cols[:, 6:7]
        dist = None
        for i in range(3):
            x = node[i : i + 1]
            w = x + time_step * node[i + 3 : i + 4]
            clear = clear - cols[:, i : i + 1] * w
            o = x - cols[:, i + 3 : i + 4]
            dist = o * o if dist is None else dist + o * o
        press = stiffness * jnp.exp(dist * (-1.0 / radius_sq)) * jnp.maximum(clear, 0.0)
        force = jnp.concatenate(
            [jnp.sum(cols[:, i : i + 1] * press, axis=0, keepdims=True) for i in range(3)], axis=0
        )
        spot = pl.ds(who * 96 + place, 3, stride=32)
        f_out[spot, :] = f_out[spot, :] + force
        return 0

    lax.fori_loop(0, lists[32, 0], pair, 0)


def return_kernel(f, r_out, ys, yr):
    g, z = lax.axis_index("grp"), lax.axis_index("dom_0")
    y, c = lax.axis_index("dom_1"), lax.axis_index("dom_2")
    turns = [(dy, dc) for dy in range(NY) for dc in range(NC) if dy or dc]
    barrier = pltpu.get_barrier_semaphore()
    for dy, dc in turns:
        pl.semaphore_signal(
            barrier, inc=1, device_id=(g, z, (y + dy) % NY, (c + dc) % NC), device_id_type=MESH
        )
    pl.semaphore_wait(barrier, len(turns))
    me = y * 2 + c
    sends = []
    for dy, dc in turns:
        k = dy * 2 + dc - 1
        to_y, to_c = (y + dy) % NY, (c + dc) % NC
        copy = pltpu.make_async_remote_copy(
            src_ref=f.at[to_y * 2 + to_c],
            dst_ref=r_out.at[me],
            send_sem=ys.at[k],
            recv_sem=yr.at[k],
            device_id=(g, z, to_y, to_c),
            device_id_type=MESH,
        )
        copy.start()
        sends.append(copy)
    r_out[me] = f[me]
    for dy, dc in turns:
        k = dy * 2 + dc - 1
        fy, fc = (y - dy + NY) % NY, (c + dc) % NC
        slot = r_out.at[fy * 2 + fc]
        pltpu.make_async_remote_copy(
            src_ref=slot,
            dst_ref=slot,
            send_sem=ys.at[k],
            recv_sem=yr.at[k],
            device_id=(g, z, fy, fc),
            device_id_type=MESH,
        ).wait_recv()
    for copy in sends:
        copy.wait_send()


def order_kernel(tgt, r_in, out):
    def one(i, _):
        out[i] = r_in[pl.ds(tgt[i], 3, stride=32), :]
        return 0

    lax.fori_loop(0, 128, one, 0, unroll=8)


def vmem():
    return pl.BlockSpec(memory_space=pltpu.VMEM)


def smem():
    return pl.BlockSpec(memory_space=pltpu.SMEM)


def shape(*dims, kind=F32):
    return jax.ShapeDtypeStruct(dims, kind)


def shards(node_state, node_dest, seg_nodes, seg_conn, pair_seg, pair_slot):
    dma = pltpu.SemaphoreType.DMA
    placed, geo, tgt = pl.pallas_call(
        prep_kernel,
        name="prep",
        out_shape=(shape(8 * 192, 128), shape(64, 128), shape(128, kind=jnp.int32)),
        in_specs=[smem()] + [vmem()] * 5,
        out_specs=(vmem(), vmem(), smem()),
        scratch_shapes=[pltpu.SMEM((128,), jnp.int32)],
    )(node_dest, node_state, seg_nodes, seg_conn, pair_seg, pair_slot)
    nodes, geos = pl.pallas_call(
        exchange_kernel,
        name="exchange",
        out_shape=(shape(8, 192, 128), shape(NX, NZ, 64, 128)),
        in_specs=[vmem()] * 2,
        out_specs=(vmem(), vmem()),
        scratch_shapes=[dma((7,)), dma((7,)), dma((15,)), dma((15,)), dma((16, 3)), dma((16, 3))],
        compiler_params=pltpu.CompilerParams(collective_id=0, has_side_effects=True),
    )(placed.reshape(8, 192, 128), geo)
    forces = pl.pallas_call(
        force_kernel,
        name="forces",
        out_shape=shape(8 * 96, 128),
        in_specs=[vmem()] * 2,
        out_specs=vmem(),
        scratch_shapes=[pltpu.VMEM((40, 128), jnp.int32), pltpu.SMEM((40, 128), jnp.int32), dma],
    )(nodes.reshape(8 * 192, 128), geos.reshape(NX * NZ * 64, 128))
    back = pl.pallas_call(
        return_kernel,
        name="giveback",
        out_shape=shape(8, 96, 128),
        in_specs=[vmem()],
        out_specs=vmem(),
        scratch_shapes=[dma((7,)), dma((7,))],
        compiler_params=pltpu.CompilerParams(collective_id=1, has_side_effects=True),
    )(forces.reshape(8, 96, 128))
    return pl.pallas_call(
        order_kernel,
        name="order",
        out_shape=shape(128, 3, 128),
        in_specs=[smem(), vmem()],
        out_specs=vmem(),
    )(tgt, back.reshape(8 * 96, 128))


def solution(mesh):
    split = Mesh(mesh.devices.reshape(NX, NZ, NY, NC), AXES)
    placed = (
        P(AXES, None, None),
        P(AXES),
        P(None, AXES),
        P(None, AXES),
        P(AXES, None, None),
        P(AXES, None, None),
    )
    return jax.shard_map(
        shards, mesh=split, in_specs=placed, out_specs=P(AXES, None, None), check_vma=False
    )
```

time: 169 us -> 122 us (0.72)
  the two profiles are of different devices: /device:TPU:1 before, /device:TPU:35 now
where the time goes in v1:
time: 122 us
  Pallas kernels  118 us (97%)
  local copies, waits for them, and re-layouts  3.65 us (3%)
    pallas_call x1, Pallas kernels, shards(): pl.pallas_call(force_kernel, name='forces', out_shape=shape(8 * 96, 128),...  49.2 us
    pallas_call x1, Pallas kernels, shards(): pl.pallas_call(exchange_kernel, name='exchange', out_shape=(shape(8, 192,...  37.1 us
    pallas_call x1, Pallas kernels, shards(): pl.pallas_call(return_kernel, name='giveback', out_shape=shape(8, 96, 128...  26.8 us
    pallas_call x1, Pallas kernels, shards(): pl.pallas_call(prep_kernel, name='prep', out_shape=(shape(8 * 192, 128),...  2.8 us

profile of v1, /device:TPU:35, one launch (start us, length us, event | category | flops | bytes accessed | tf_op | source)
XLA Modules:
  0.0 121.6 jit_solution(12239052080881273219)
XLA Ops:
  0.0 2.0 %copy.7.node = f32[128,6,128]{2,1,0:T(8,128)} copy(f32[128,6,128]{2,0,1:T(8,128)} %param.6) | data formatting | bytes 786432 | tf_op args[0]
  2.0 2.8 %prep.1 = (f32[1536,128]{1,0:T(8,128)}, f32[64,128]{1,0:T(8,128)}, s32[128]{0:T(128)}) custom-call(s32[128]{0:T(128)} %dest.1, f32[128,6,128]{2,1,0:T(8,128)} %copy.7.node, f32[6,512]{1,0:T(8,128)} %seg_nodes.1, s32[3,1024]{1,0:T(4,128)} %conn.1, s32[1,4,32]{2,1,0:T(4,128)} %pseg.1, s32[1,4,32]{2,1,0:T(4,128)} %pslot.1), custom_call_target="tpu_custom_call" | custom-call | tf_op jit(solution)/shard_map/prep/pallas_call | solution.py:310
  4.8 37.1 %exchange.1 = (f32[8,192,128]{2,1,0:T(8,128)}, f32[4,16,64,128]{3,2,1,0:T(8,128)}) custom-call(f32[8,192,128]{2,1,0:T(8,128)} %bitcast.8, f32[64,128]{1,0:T(8,128)} %get-tuple-element.12.geo), custom_call_target="tpu_custom_call" | custom-call | tf_op jit(solution)/shard_map/exchange/pallas_call | solution.py:318
  41.9 49.2 %forces.1 = f32[768,128]{1,0:T(8,128)} custom-call(f32[1536,128]{1,0:T(8,128)} %bitcast.9, f32[4096,128]{1,0:T(8,128)} %bitcast.5), custom_call_target="tpu_custom_call" | custom-call | tf_op jit(solution)/shard_map/forces/pallas_call | solution.py:327
  91.1 26.8 %giveback.1 = f32[8,96,128]{2,1,0:T(8,128)} custom-call(f32[8,96,128]{2,1,0:T(8,128)} %bitcast.6), custom_call_target="tpu_custom_call" | custom-call | tf_op jit(solution)/shard_map/giveback/pallas_call | solution.py:335
  118.0 2.0 %order.1 = f32[128,3,128]{2,1,0:T(4,128)} custom-call(s32[128]{0:T(128)} %get-tuple-element.10.tgt, f32[768,128]{1,0:T(8,128)} %bitcast.7), custom_call_target="tpu_custom_call" | custom-call | tf_op jit(solution)/shard_map/order/pallas_call | solution.py:344
  120.0 1.6 %copy.8 = f32[128,3,128]{2,0,1:T(8,128)} copy(f32[128,3,128]{2,1,0:T(4,128)} %order.1) | data formatting | bytes 393216 | tf_op jit(solution)/shard_map/order/pallas_call | solution.py:344

commit v2 on v1

v2 whole, which is shorter than its diff:
```python
import math

import jax
import jax.numpy as jnp
from jax import lax
from jax.experimental import pallas as pl
from jax.experimental.pallas import tpu as pltpu
from jax.sharding import Mesh
from jax.sharding import PartitionSpec as P

AXES = ("grp", "dom_0", "dom_1", "dom_2")
NX, NZ, NY, NC = 4, 16, 4, 2
MESH = pl.DeviceIdType.MESH
REACH = 3
BATCH = 8
F32, BF16, I32 = jnp.float32, jnp.bfloat16, jnp.int32

time_step = 0.5
stiffness = 0.5
radius_sq = 0.5
root = math.sqrt(math.log2(math.e) / radius_sq)

TURNS = [(a, b, c) for a in range(NX) for b in range(NY) for c in range(NC) if a or b or c]


def prep_kernel(dest, node, seg_nodes, conn, pseg, pslot, s_out, geo, tgt, cnt, xw):
    def clear(i, _):
        cnt[i] = 0
        return 0

    lax.fori_loop(0, 128, clear, 0, unroll=16)
    x = node[0:384, :]
    xw[0:384, :] = x * root
    xw[384:768, :] = x + time_step * node[384:768, :]

    def place(i, _):
        d = dest[i]
        k = cnt[d]
        cnt[d] = k + 1
        z = lax.shift_right_logical(d, 3)
        p = (z & 3) * 8 + (d & 7)
        slot = lax.shift_right_logical(z, 2) * 2 + k
        s_out[pl.ds(p * 48 + slot, 6, stride=8), :] = xw[pl.ds(i, 6, stride=128), :]
        tgt[i] = p * 24 + slot
        return 0

    lax.fori_loop(0, 128, place, 0, unroll=8)

    corners = []
    for k in range(3):
        idx = jnp.concatenate([conn[k : k + 1, b * 128 : (b + 1) * 128] for b in range(8)], axis=0)
        hi = lax.shift_right_logical(idx, 7)
        lo = lax.bitwise_and(idx, 127)
        comps = []
        for i in range(6):
            got = None
            for q in range(4):
                table = jnp.broadcast_to(seg_nodes[i : i + 1, q * 128 : (q + 1) * 128], (8, 128))
                part = jnp.take_along_axis(table, lo, axis=1)
                got = part if got is None else jnp.where(hi == q, part, got)
            comps.append(got)
        corners.append(comps)
    a, b, c = corners
    e1 = [b[i] - a[i] for i in range(3)]
    e2 = [c[i] - a[i] for i in range(3)]
    n = [0.5 * (e1[(i + 1) % 3] * e2[(i + 2) % 3] - e1[(i + 2) % 3] * e2[(i + 1) % 3]) for i in range(3)]
    m = [(a[i] + b[i] + c[i]) / 3.0 for i in range(3)]
    u = [(a[i + 3] + b[i + 3] + c[i + 3]) / 3.0 for i in range(3)]
    off = sum(n[i] * (m[i] + time_step * u[i]) for i in range(3))
    values = [2.0 * root * v for v in m] + [-stiffness * v for v in n] + [stiffness * off]
    for i, v in enumerate(values):
        geo[pl.ds(i, 8, stride=8), :] = v
    tables = []
    for tab in (pseg, pslot):
        t = jnp.concatenate([tab[0].astype(F32), jnp.zeros((4, 96), F32)], axis=1)
        rows = [pltpu.roll(jnp.broadcast_to(t[r : r + 1], (8, 128)), 32 * r, 1) for r in range(4)]
        tables.append(rows[0] + rows[1] + rows[2] + rows[3])
    sub = lax.broadcasted_iota(I32, (8, 128), 0)
    geo[pl.ds(7, 8, stride=8), :] = jnp.where(sub == 0, tables[0], tables[1])


def start(src, dst, ss, rs, dev):
    copy = pltpu.make_async_remote_copy(
        src_ref=src, dst_ref=dst, send_sem=ss, recv_sem=rs, device_id=dev, device_id_type=MESH
    )
    copy.start()
    return copy


def landed(dst, ss, rs, dev):
    pltpu.make_async_remote_copy(
        src_ref=dst, dst_ref=dst, send_sem=ss, recv_sem=rs, device_id=dev, device_id_type=MESH
    ).wait_recv()


def exchange_kernel(s, geo, n_out, g_out, ys, yr, zs, zr, ws, wr):
    g, z = lax.axis_index("grp"), lax.axis_index("dom_0")
    y, c = lax.axis_index("dom_1"), lax.axis_index("dom_2")

    def zat(k):
        return (z + k + NZ) % NZ

    quad = z % 4
    other = (quad, z - quad + g, y, c)
    diagonal = quad == g
    peers = [((g + a) % NX, z, (y + b) % NY, (c + e) % NC) for a, b, e in TURNS]
    for e in range(1, REACH + 1):
        peers += [(g, zat(e), y, c), (g, zat(-e), y, c)]
    barrier = pltpu.get_barrier_semaphore()
    for peer in peers:
        pl.semaphore_signal(barrier, inc=1, device_id=peer, device_id_type=MESH)

    @pl.when(jnp.logical_not(diagonal))
    def _():
        pl.semaphore_signal(barrier, inc=1, device_id=other, device_id_type=MESH)

    pl.semaphore_wait(barrier, len(peers) + jnp.where(diagonal, 0, 1))
    me = g * 8 + y * 2 + c

    @pl.when(jnp.logical_not(diagonal))
    def _():
        start(geo, g_out.at[other[1]], ws, wr, other)

    def node_send(k):
        a, b, e = TURNS[k]
        dev = ((g + a) % NX, z, (y + b) % NY, (c + e) % NC)
        start(s.at[dev[0] * 8 + dev[2] * 2 + dev[3]], n_out.at[me], ys.at[k], yr.at[k], dev)

    def number(sign, d):
        return (d if sign > 0 else 8 + d) - 1

    most = {1: 8, -1: 7}

    def forward_z(sign, p, src):
        for e in range(1, REACH + 1):
            if p + e <= most[sign]:
                k = number(sign, p + e)
                start(src, g_out.at[zat(-sign * p)], zs.at[k], zr.at[k], (g, zat(sign * e), y, c))

    first = 12
    for k in range(first):
        node_send(k)

    @pl.when(diagonal)
    def _():
        forward_z(1, 0, geo)
        forward_z(-1, 0, geo)
        g_out[z] = geo[...]

    @pl.when(jnp.logical_not(diagonal))
    def _():
        landed(g_out.at[z], ws, wr, other)
        forward_z(1, 0, g_out.at[z])
        forward_z(-1, 0, g_out.at[z])

    for k in range(first, len(TURNS)):
        node_send(k)
    n_out[me] = s[me]

    for d in range(1, 9):
        for sign in (1, -1):
            if d <= most[sign]:
                k = number(sign, d)
                hop = d - ((d - 1) // REACH) * REACH
                slot = g_out.at[zat(-sign * d)]
                landed(slot, zs.at[k], zr.at[k], (g, zat(-sign * hop), y, c))
                if d % REACH == 0:
                    forward_z(sign, d, slot)
    for k, (a, b, e) in enumerate(TURNS):
        dev = ((g - a + NX) % NX, z, (y - b + NY) % NY, (c + e) % NC)
        landed(n_out.at[dev[0] * 8 + dev[2] * 2 + dev[3]], ys.at[k], yr.at[k], dev)

    def left(src, ss, rs, dev):
        pltpu.make_async_remote_copy(
            src_ref=src, dst_ref=src, send_sem=ss, recv_sem=rs, device_id=dev, device_id_type=MESH
        ).wait_send()

    for k, (a, b, e) in enumerate(TURNS):
        dev = ((g + a) % NX, z, (y + b) % NY, (c + e) % NC)
        left(s.at[dev[0] * 8 + dev[2] * 2 + dev[3]], ys.at[k], yr.at[k], dev)
    for sign in (1, -1):
        for d in range(1, most[sign] + 1):
            k = number(sign, d)
            p = ((d - 1) // REACH) * REACH
            left(g_out.at[zat(-sign * p)], zs.at[k], zr.at[k], (g, zat(sign * (d - p)), y, c))

    @pl.when(jnp.logical_not(diagonal))
    def _():
        left(geo, ws, wr, other)


def split3(t):
    a = t.astype(BF16).astype(F32)
    r = t - a
    b = r.astype(BF16).astype(F32)
    return a, b, r - b


def force_kernel(n_in, g_in, f_out, lists_v, lists, sem):
    z = lax.axis_index("dom_0")
    seg = g_in[pl.ds(7, 16, stride=64), :]
    slot = g_in[pl.ds(15, 16, stride=64), :].astype(I32)
    lane = lax.broadcasted_iota(I32, (16, 128), 1)
    sub = lax.broadcasted_iota(I32, (16, 128), 0)
    hit = lax.shift_right_logical(slot, 4) == z
    mask = jnp.where(hit, 1.0, 0.0).astype(F32)
    low4 = lax.bitwise_and(slot, 15)
    code_a = seg + (sub * 8).astype(F32)
    who = lax.shift_right_logical(lane, 5) * 8 + lax.shift_right_logical(low4, 1)
    spot8 = lax.shift_right_logical(sub, 2) * 2 + lax.bitwise_and(low4, 1)
    code_b = (who * 8 + spot8).astype(F32)
    i0 = lax.broadcasted_iota(I32, (128, 128), 0)
    i1 = lax.broadcasted_iota(I32, (128, 128), 1)
    before = jnp.where(i0 < i1, 1.0, 0.0).astype(F32)
    inner = jnp.dot(mask, before, preferred_element_type=F32)
    total = jnp.dot(mask, jnp.ones((128, 128), F32), preferred_element_type=F32)
    j0 = lax.broadcasted_iota(I32, (16, 16), 0)
    j1 = lax.broadcasted_iota(I32, (16, 16), 1)
    above = jnp.dot(jnp.where(j1 < j0, 1.0, 0.0).astype(F32), total, preferred_element_type=F32)
    pos = (inner + above).astype(I32)
    high = jnp.where(hit, lax.shift_right_logical(pos, 7), -1)
    low = lax.bitwise_and(pos, 127)
    packed = jnp.zeros((32, 128), F32)
    for i in range(16):
        at = high[i : i + 1] == sub
        left = jnp.concatenate(
            [jnp.where(at, code_a[i : i + 1], 0.0), jnp.where(at, code_b[i : i + 1], 0.0)], axis=0
        )
        spot = jnp.where(low[i : i + 1] == i0, 1.0, 0.0).astype(F32)
        packed = packed + lax.dot_general(left, spot, (((1,), (1,)), ((), ())), preferred_element_type=F32)
    count = (total[15:16] + above[15:16]).astype(I32)
    code = packed[16:32].astype(I32)
    who = lax.shift_right_logical(code, 3)
    spot8 = lax.bitwise_and(code, 7)
    lists_v[0:16, :] = packed[0:16].astype(I32) * 8
    lists_v[16:32, :] = who * 48 + spot8
    lists_v[32:48, :] = jnp.where(sub * 128 + lane < count, who * 24 + spot8, 32 * 24)
    lists_v[48:56, :] = jnp.broadcast_to(count, (8, 128))
    copy = pltpu.make_async_copy(lists_v, lists, sem)
    copy.start()
    f_out[...] = jnp.zeros_like(f_out)
    copy.wait()

    row = lax.broadcasted_iota(I32, (8, 128), 0)
    ones = jnp.ones((8, 128), F32)
    blank = jnp.zeros((48, 128), BF16)

    def node_side(at):
        t = n_in[pl.ds(at, 6, stride=8), :]
        x0, x1, x2 = t[0:1], t[1:2], t[2:3]
        q = -(x0 * x0 + x1 * x1 + x2 * x2)
        full = jnp.concatenate([t, ones[0:1], q], axis=0)
        a, b, e = split3(full)
        return jnp.concatenate([a, b, a, e, a, b], axis=0).astype(BF16)

    def seg_side(at):
        t = g_in[pl.ds(pl.multiple_of(at, 8), 8), :]
        m0, m1, m2 = t[0:1], t[1:2], t[2:3]
        q = -0.25 * (m0 * m0 + m1 * m1 + m2 * m2)
        dist = jnp.where(row < 3, t, jnp.where(row == 6, q, jnp.where(row == 7, 1.0, 0.0)))
        clear = jnp.where((row >= 3) & (row <= 6), t, 0.0)
        sides = []
        for v in (dist, clear):
            a, b, e = split3(v)
            sides.append(jnp.concatenate([a, a, b, a, e, b], axis=0))
        a = t.astype(BF16).astype(F32)
        return sides[0], sides[1], a, t - a

    def two(p):
        out = []
        for i in range(2):
            q = p + i
            hi, lo = lax.shift_right_logical(q, 7), lax.bitwise_and(q, 127)
            out.append((lists[hi, lo], lists[16 + hi, lo], lists[32 + hi, lo]))
        na, nb = node_side(out[0][1]), node_side(out[1][1])
        rhs = jnp.concatenate(
            [jnp.concatenate([na, blank], axis=1), jnp.concatenate([blank, nb], axis=1)], axis=0
        )
        da, ca, ha, la = seg_side(out[0][0])
        db, cb, hb, lb = seg_side(out[1][0])
        dist = jnp.concatenate([da, db], axis=0).T.astype(BF16)
        clear = jnp.concatenate([ca, cb], axis=0).T.astype(BF16)
        e = jnp.dot(dist, rhs, preferred_element_type=F32)
        w = jnp.dot(clear, rhs, preferred_element_type=F32)
        press = jnp.exp2(e) * jnp.maximum(w, 0.0)
        p_hi = press.astype(BF16)
        p_lo = (press - p_hi.astype(F32)).astype(BF16)
        nothing = jnp.zeros((8, 128), F32)
        left = jnp.concatenate(
            [
                jnp.concatenate([ha, ha], axis=1),
                jnp.concatenate([la, nothing], axis=1),
                jnp.concatenate([hb, hb], axis=1),
                jnp.concatenate([lb, nothing], axis=1),
            ],
            axis=0,
        ).astype(BF16)
        f = jnp.dot(left, jnp.concatenate([p_hi, p_lo], axis=0), preferred_element_type=F32)
        fa = -2.0 * (f[0:8, 0:128] + f[8:16, 0:128])
        fb = -2.0 * (f[16:24, 128:256] + f[24:32, 128:256])
        return [(out[0][2], fa[3:6]), (out[1][2], fb[3:6])]

    def batch(i, _):
        done = []
        for j in range(0, BATCH, 2):
            done += two(i * BATCH + j)
        for at, f in done:
            here = pl.ds(at, 3, stride=8)
            f_out[here, :] = f_out[here, :] + f
        return 0

    lax.fori_loop(0, (lists[48, 0] + BATCH - 1) // BATCH, batch, 0)


def return_kernel(f, r_out, ys, yr):
    g, z = lax.axis_index("grp"), lax.axis_index("dom_0")
    y, c = lax.axis_index("dom_1"), lax.axis_index("dom_2")
    barrier = pltpu.get_barrier_semaphore()
    for a, b, e in TURNS:
        pl.semaphore_signal(
            barrier, inc=1, device_id=((g + a) % NX, z, (y + b) % NY, (c + e) % NC), device_id_type=MESH
        )
    pl.semaphore_wait(barrier, len(TURNS))
    me = g * 8 + y * 2 + c
    sends = []
    for k, (a, b, e) in enumerate(TURNS):
        dev = ((g + a) % NX, z, (y + b) % NY, (c + e) % NC)
        sends.append(start(f.at[dev[0] * 8 + dev[2] * 2 + dev[3]], r_out.at[me], ys.at[k], yr.at[k], dev))
    r_out[me] = f[me]
    for k, (a, b, e) in enumerate(TURNS):
        dev = ((g - a + NX) % NX, z, (y - b + NY) % NY, (c + e) % NC)
        landed(r_out.at[dev[0] * 8 + dev[2] * 2 + dev[3]], ys.at[k], yr.at[k], dev)
    for copy in sends:
        copy.wait_send()


def order_kernel(tgt, r_in, out):
    def one(i, _):
        out[pl.ds(i, 3, stride=128), :] = r_in[pl.ds(tgt[i], 3, stride=8), :]
        return 0

    lax.fori_loop(0, 128, one, 0, unroll=8)


def vmem():
    return pl.BlockSpec(memory_space=pltpu.VMEM)


def smem():
    return pl.BlockSpec(memory_space=pltpu.SMEM)


def shape(*dims, kind=F32):
    return jax.ShapeDtypeStruct(dims, kind)


def shards(node_state, node_dest, seg_nodes, seg_conn, pair_seg, pair_slot):
    dma = pltpu.SemaphoreType.DMA
    many = len(TURNS)
    nodes = jnp.transpose(node_state, (1, 0, 2)).reshape(768, 128)
    placed, geo, tgt = pl.pallas_call(
        prep_kernel,
        name="prep",
        out_shape=(shape(32 * 48, 128), shape(64, 128), shape(128, kind=I32)),
        in_specs=[smem()] + [vmem()] * 5,
        out_specs=(vmem(), vmem(), smem()),
        scratch_shapes=[pltpu.SMEM((128,), I32), pltpu.VMEM((768, 128), F32)],
    )(node_dest, nodes, seg_nodes, seg_conn, pair_seg, pair_slot)
    met, geos = pl.pallas_call(
        exchange_kernel,
        name="exchange",
        out_shape=(shape(32, 48, 128), shape(NZ, 64, 128)),
        in_specs=[vmem()] * 2,
        out_specs=(vmem(), vmem()),
        scratch_shapes=[dma((many,)), dma((many,)), dma((15,)), dma((15,)), dma, dma],
        compiler_params=pltpu.CompilerParams(collective_id=0, has_side_effects=True),
    )(placed.reshape(32, 48, 128), geo)
    forces = pl.pallas_call(
        force_kernel,
        name="forces",
        out_shape=shape(33 * 24, 128),
        in_specs=[vmem()] * 2,
        out_specs=vmem(),
        scratch_shapes=[pltpu.VMEM((56, 128), I32), pltpu.SMEM((56, 128), I32), dma],
    )(met.reshape(32 * 48, 128), geos.reshape(NZ * 64, 128))
    back = pl.pallas_call(
        return_kernel,
        name="giveback",
        out_shape=shape(32, 24, 128),
        in_specs=[vmem()],
        out_specs=vmem(),
        scratch_shapes=[dma((many,)), dma((many,))],
        compiler_params=pltpu.CompilerParams(collective_id=1, has_side_effects=True),
    )(forces.reshape(33, 24, 128))
    rows = pl.pallas_call(
        order_kernel,
        name="order",
        out_shape=shape(384, 128),
        in_specs=[smem(), vmem()],
        out_specs=vmem(),
    )(tgt, back.reshape(32 * 24, 128))
    return jnp.transpose(rows.reshape(3, 128, 128), (1, 0, 2))


def solution(mesh):
    split = Mesh(mesh.devices.reshape(NX, NZ, NY, NC), AXES)
    placed = (
        P(AXES, None, None),
        P(AXES),
        P(None, AXES),
        P(None, AXES),
        P(AXES, None, None),
        P(AXES, None, None),
    )
    return jax.shard_map(
        shards, mesh=split, in_specs=placed, out_specs=P(AXES, None, None), check_vma=False
    )
```

time: 122 us -> 80.7 us (0.66)
  the two profiles are of different devices: /device:TPU:35 before, /device:TPU:1 now
where the time goes in v2:
time: 80.7 us; the launch traced here: 80.5 us
  Pallas kernels  80.5 us (100%)
    pallas_call x1, Pallas kernels, shards(): pl.pallas_call(exchange_kernel, name='exchange', out_shape=(shape(32, 48,...  39.3 us
    pallas_call x1, Pallas kernels, shards(): pl.pallas_call(force_kernel, name='forces', out_shape=shape(33 * 24, 128)...  19.5 us
    pallas_call x1, Pallas kernels, shards(): pl.pallas_call(return_kernel, name='giveback', out_shape=shape(32, 24, 12...  16.8 us
    pallas_call x1, Pallas kernels, shards(): pl.pallas_call(prep_kernel, name='prep', out_shape=(shape(32 * 48, 128),...  2.89 us
    pallas_call x1, Pallas kernels, shards(): pl.pallas_call(order_kernel, name='order', out_shape=shape(384, 128), in_...  1.97 us

profile of v2, /device:TPU:1, one launch (start us, length us, event | category | flops | bytes accessed | tf_op | source)
XLA Modules:
  0.0 80.5 jit_solution(6929853324343668929)
XLA Ops:
  0.0 2.9 %prep.1 = (f32[1536,128]{1,0:T(8,128)}, f32[64,128]{1,0:T(8,128)}, s32[128]{0:T(128)}) custom-call(s32[128]{0:T(128)} %dest.1, f32[768,128]{1,0:T(8,128)} %bitcast.16, f32[6,512]{1,0:T(8,128)} %seg_nodes.1, s32[3,1024]{1,0:T(4,128)} %conn.1, s32[1,4,32]{2,1,0:T(4,128)} %pseg.1, s32[1,4,32]{2,1,0:T(4,128)} %pslot.1), custom_call_target="tpu_custom_call" | custom-call | tf_op jit(solution)/shard_map/prep/pallas_call | solution.py:361
  2.9 39.3 %exchange.1 = (f32[32,48,128]{2,1,0:T(8,128)}, f32[16,64,128]{2,1,0:T(8,128)}) custom-call(f32[32,48,128]{2,1,0:T(8,128)} %bitcast.13, f32[64,128]{1,0:T(8,128)} %get-tuple-element.12.geo), custom_call_target="tpu_custom_call" | custom-call | tf_op jit(solution)/shard_map/exchange/pallas_call | solution.py:369
  42.2 19.5 %forces.1 = f32[792,128]{1,0:T(8,128)} custom-call(f32[1536,128]{1,0:T(8,128)} %bitcast.14, f32[1024,128]{1,0:T(8,128)} %bitcast.15), custom_call_target="tpu_custom_call" | custom-call | tf_op jit(solution)/shard_map/forces/pallas_call | solution.py:378
  61.7 16.8 %giveback.1 = f32[32,24,128]{2,1,0:T(8,128)} custom-call(f32[33,24,128]{2,1,0:T(8,128)} %bitcast.11), custom_call_target="tpu_custom_call" | custom-call | tf_op jit(solution)/shard_map/giveback/pallas_call | solution.py:386
  78.5 2.0 %order.1 = f32[384,128]{1,0:T(8,128)} custom-call(s32[128]{0:T(128)} %get-tuple-element.10.tgt, f32[768,128]{1,0:T(8,128)} %bitcast.12), custom_call_target="tpu_custom_call" | custom-call | tf_op jit(solution)/shard_map/order/pallas_call | solution.py:395

commit v3 on v2

--- a/solution.py
+++ b/solution.py
@@ -12,7 +12,8 @@
 NX, NZ, NY, NC = 4, 16, 4, 2
 MESH = pl.DeviceIdType.MESH
 REACH = 3
-BATCH = 8
+BATCH = 16
+ROOM = 16 << 20
 F32, BF16, I32 = jnp.float32, jnp.bfloat16, jnp.int32
 
 time_step = 0.5
@@ -266,7 +267,7 @@
         a = t.astype(BF16).astype(F32)
         return sides[0], sides[1], a, t - a
 
-    def two(p):
+    def build(p):
         out = []
         for i in range(2):
             q = p + i
@@ -280,11 +281,6 @@
         db, cb, hb, lb = seg_side(out[1][0])
         dist = jnp.concatenate([da, db], axis=0).T.astype(BF16)
         clear = jnp.concatenate([ca, cb], axis=0).T.astype(BF16)
-        e = jnp.dot(dist, rhs, preferred_element_type=F32)
-        w = jnp.dot(clear, rhs, preferred_element_type=F32)
-        press = jnp.exp2(e) * jnp.maximum(w, 0.0)
-        p_hi = press.astype(BF16)
-        p_lo = (press - p_hi.astype(F32)).astype(BF16)
         nothing = jnp.zeros((8, 128), F32)
         left = jnp.concatenate(
             [
@@ -295,18 +291,28 @@
             ],
             axis=0,
         ).astype(BF16)
-        f = jnp.dot(left, jnp.concatenate([p_hi, p_lo], axis=0), preferred_element_type=F32)
-        fa = -2.0 * (f[0:8, 0:128] + f[8:16, 0:128])
-        fb = -2.0 * (f[16:24, 128:256] + f[24:32, 128:256])
-        return [(out[0][2], fa[3:6]), (out[1][2], fb[3:6])]
+        return dist, clear, rhs, left, out[0][2], out[1][2]
+
+    def pressure(e, w):
+        press = jnp.exp2(e) * jnp.maximum(w, 0.0)
+        p_hi = press.astype(BF16)
+        p_lo = (press - p_hi.astype(F32)).astype(BF16)
+        return jnp.concatenate([p_hi, p_lo], axis=0)
 
     def batch(i, _):
-        done = []
-        for j in range(0, BATCH, 2):
-            done += two(i * BATCH + j)
-        for at, f in done:
-            here = pl.ds(at, 3, stride=8)
-            f_out[here, :] = f_out[here, :] + f
+        made = [build(i * BATCH + j) for j in range(0, BATCH, 2)]
+        ew = [
+            (jnp.dot(m[0], m[2], preferred_element_type=F32), jnp.dot(m[1], m[2], preferred_element_type=F32))
+            for m in made
+        ]
+        ps = [pressure(e, w) for e, w in ew]
+        fs = [jnp.dot(m[3], p, preferred_element_type=F32) for m, p in zip(made, ps)]
+        for m, f in zip(made, fs):
+            fa = -2.0 * (f[0:8, 0:128] + f[8:16, 0:128])
+            fb = -2.0 * (f[16:24, 128:256] + f[24:32, 128:256])
+            for at, v in ((m[4], fa[3:6]), (m[5], fb[3:6])):
+                here = pl.ds(at, 3, stride=8)
+                f_out[here, :] = f_out[here, :] + v
         return 0
 
     lax.fori_loop(0, (lists[48, 0] + BATCH - 1) // BATCH, batch, 0)
@@ -365,6 +371,7 @@
         in_specs=[smem()] + [vmem()] * 5,
         out_specs=(vmem(), vmem(), smem()),
         scratch_shapes=[pltpu.SMEM((128,), I32), pltpu.VMEM((768, 128), F32)],
+        compiler_params=pltpu.CompilerParams(vmem_limit_bytes=ROOM),
     )(node_dest, nodes, seg_nodes, seg_conn, pair_seg, pair_slot)
     met, geos = pl.pallas_call(
         exchange_kernel,
@@ -373,7 +380,7 @@
         in_specs=[vmem()] * 2,
         out_specs=(vmem(), vmem()),
         scratch_shapes=[dma((many,)), dma((many,)), dma((15,)), dma((15,)), dma, dma],
-        compiler_params=pltpu.CompilerParams(collective_id=0, has_side_effects=True),
+        compiler_params=pltpu.CompilerParams(collective_id=0, has_side_effects=True, vmem_limit_bytes=ROOM),
     )(placed.reshape(32, 48, 128), geo)
     forces = pl.pallas_call(
         force_kernel,
@@ -382,6 +389,7 @@
         in_specs=[vmem()] * 2,
         out_specs=vmem(),
         scratch_shapes=[pltpu.VMEM((56, 128), I32), pltpu.SMEM((56, 128), I32), dma],
+        compiler_params=pltpu.CompilerParams(vmem_limit_bytes=ROOM),
     )(met.reshape(32 * 48, 128), geos.reshape(NZ * 64, 128))
     back = pl.pallas_call(
         return_kernel,
@@ -390,7 +398,7 @@
         in_specs=[vmem()],
         out_specs=vmem(),
         scratch_shapes=[dma((many,)), dma((many,))],
-        compiler_params=pltpu.CompilerParams(collective_id=1, has_side_effects=True),
+        compiler_params=pltpu.CompilerParams(collective_id=1, has_side_effects=True, vmem_limit_bytes=ROOM),
     )(forces.reshape(33, 24, 128))
     rows = pl.pallas_call(
         order_kernel,
@@ -398,6 +406,7 @@
         out_shape=shape(384, 128),
         in_specs=[smem(), vmem()],
         out_specs=vmem(),
+        compiler_params=pltpu.CompilerParams(vmem_limit_bytes=ROOM),
     )(tgt, back.reshape(32 * 24, 128))
     return jnp.transpose(rows.reshape(3, 128, 128), (1, 0, 2))
 

time: 80.7 us -> 69 us (0.86)
  Pallas kernels: 80.5 us -> 63.9 us
  local copies, waits for them, and re-layouts: 0 us -> 4.45 us
    pallas_call x1, Pallas kernels: 19.5 us -> 7.84 us  [shards(): pl.pallas_call(force_kernel, name='forces', out_shape=shape(33 * 24, 128)...]
    unnamed x0 -> x12, local copies, waits for them, and re-layouts: none -> 4.45 us
    pallas_call x1, Pallas kernels: 39.3 us -> 37.2 us  [shards(): pl.pallas_call(exchange_kernel, name='exchange', out_shape=(shape(32, 48,...]
    pallas_call x1, Pallas kernels: 16.8 us -> 15.2 us  [shards(): pl.pallas_call(return_kernel, name='giveback', out_shape=shape(32, 24, 12...]
where the time goes in v3:
time: 69 us; the launch traced here: 68.4 us
  Pallas kernels  63.9 us (93%)
  local copies, waits for them, and re-layouts  4.45 us (6%)
    pallas_call x1, Pallas kernels, shards(): pl.pallas_call(exchange_kernel, name='exchange', out_shape=(shape(32, 48,...  37.2 us
    pallas_call x1, Pallas kernels, shards(): pl.pallas_call(return_kernel, name='giveback', out_shape=shape(32, 24, 12...  15.2 us
    pallas_call x1, Pallas kernels, shards(): pl.pallas_call(force_kernel, name='forces', out_shape=shape(33 * 24, 128)...  7.84 us
    unnamed x12, local copies, waits for them, and re-layouts  4.45 us
    pallas_call x1, Pallas kernels, shards(): pl.pallas_call(prep_kernel, name='prep', out_shape=(shape(32 * 48, 128),...  2.12 us
    pallas_call x1, Pallas kernels, shards(): pl.pallas_call(order_kernel, name='order', out_shape=shape(384, 128), in_...  1.5 us

profile of v3, /device:TPU:1, one launch (start us, length us, event | category | flops | bytes accessed | tf_op | source)
XLA Modules:
  0.0 68.4 jit_solution(11862076423038674743)
XLA Ops:
  0.0 0.0 copy-start.5
  0.0 0.7 copy-done.5
  0.7 0.0 copy-start
  0.7 1.0 %copy-done = f32[128,6,128]{2,0,1:T(8,128)S(1)} copy-done((f32[128,6,128]{2,0,1:T(8,128)S(1)}, f32[128,6,128]{2,0,1:T(8,128)}, u32[]{:S(2)}) %copy-start) | copy-done | bytes 393240
  1.7 0.0 copy-start.1
  1.7 0.7 %copy-done.1 = f32[6,512]{1,0:T(8,128)S(1)} copy-done((f32[6,512]{1,0:T(8,128)S(1)}, f32[6,512]{1,0:T(8,128)}, u32[]{:S(2)}) %copy-start.1) | copy-done | bytes 12312
  2.4 0.0 copy-start.2
  2.4 0.7 %copy-done.2 = s32[3,1024]{1,0:T(4,128)S(1)} copy-done((s32[3,1024]{1,0:T(4,128)S(1)}, s32[3,1024]{1,0:T(4,128)}, u32[]{:S(2)}) %copy-start.2) | copy-done | bytes 12312
  3.1 0.0 copy-start.3
  3.1 0.7 copy-done.3
  3.8 0.0 copy-start.4
  3.8 0.7 copy-done.4
  4.5 2.1 %prep.1 = (f32[1536,128]{1,0:T(8,128)S(1)}, f32[64,128]{1,0:T(8,128)S(1)}, s32[128]{0:T(128)S(1)}) custom-call(s32[128]{0:T(128)S(1)} %copy-done.5, f32[768,128]{1,0:T(8,128)S(1)} %bitcast.16, f32[6,512]{1,0:T(8,128)S(1)} %copy-done.1, s32[3,1024]{1,0:T(4,128)S(1)} %copy-done.2, s32[1,4,32]{2,1,0:T(4,128)S(1)} %copy-done.3, s32[1,4,32]{2,1,0:T(4,128)S(1)} %copy-done.4), custom_call_target="tpu_custom_call" | custom-call | tf_op jit(solution)/shard_map/prep/pallas_call | solution.py:367
  6.6 37.2 %exchange.1 = (f32[32,48,128]{2,1,0:T(8,128)S(1)}, f32[16,64,128]{2,1,0:T(8,128)S(1)}) custom-call(f32[32,48,128]{2,1,0:T(8,128)S(1)} %bitcast.13, f32[64,128]{1,0:T(8,128)S(1)} %get-tuple-element.12.geo), custom_call_target="tpu_custom_call" | custom-call | tf_op jit(solution)/shard_map/exchange/pallas_call | solution.py:376
  43.8 7.8 %forces.1 = f32[792,128]{1,0:T(8,128)S(1)} custom-call(f32[1536,128]{1,0:T(8,128)S(1)} %bitcast.14, f32[1024,128]{1,0:T(8,128)S(1)} %bitcast.15), custom_call_target="tpu_custom_call" | custom-call | tf_op jit(solution)/shard_map/forces/pallas_call | solution.py:385
  51.6 15.2 %giveback.1 = f32[32,24,128]{2,1,0:T(8,128)S(1)} custom-call(f32[33,24,128]{2,1,0:T(8,128)S(1)} %bitcast.11), custom_call_target="tpu_custom_call" | custom-call | tf_op jit(solution)/shard_map/giveback/pallas_call | solution.py:394
  66.9 1.5 %order.1 = f32[384,128]{1,0:T(8,128)} custom-call(s32[128]{0:T(128)S(1)} %get-tuple-element.10.tgt, f32[768,128]{1,0:T(8,128)S(1)} %bitcast.12), custom_call_target="tpu_custom_call" | custom-call | tf_op jit(solution)/shard_map/order/pallas_call | solution.py:403
Async XLA Ops:
  0.0 0.7 copy-start.5
  0.7 1.0 %copy-start = (f32[128,6,128]{2,0,1:T(8,128)S(1)}, f32[128,6,128]{2,0,1:T(8,128)}, u32[]{:S(2)}) copy-start(f32[128,6,128]{2,0,1:T(8,128)} %param.6) | copy-start | bytes 1179652
  1.7 0.7 %copy-start.1 = (f32[6,512]{1,0:T(8,128)S(1)}, f32[6,512]{1,0:T(8,128)}, u32[]{:S(2)}) copy-start(f32[6,512]{1,0:T(8,128)} %seg_nodes.1) | copy-start | bytes 36868
  2.4 0.7 %copy-start.2 = (s32[3,1024]{1,0:T(4,128)S(1)}, s32[3,1024]{1,0:T(4,128)}, u32[]{:S(2)}) copy-start(s32[3,1024]{1,0:T(4,128)} %conn.1) | copy-start | bytes 36868
  3.1 0.7 copy-start.3
  3.8 0.7 copy-start.4
